TPU v7x, 512 devices: a whole 4x8x8 slice. The times are simulated.
512 devices in a mesh: ta: 64 (over y, x, core), gz: 8 (over z).
Axes of the slice: x: 4, y: 8, z: 8, core: 2. Of those that a mesh axis runs over, the one named last changes fastest.
Arguments:
- time_links: float32 [2, 3, 3, 128, 32, 256], P(None, None, None, 'ta', 'gz'), may hold values from -1 to 1, as said below
- space_links: float32 [3, 2, 3, 3, 128, 32, 256], P(None, None, None, None, 'ta', 'gz'), may hold values from -1 to 1, as said below
Outputs:
- gauge: float32 [2, 3, 3, 128, 32, 256], P(None, None, None, 'ta', 'gz')
- links_fixed: float32 [3, 2, 3, 3, 128, 32, 256], P(None, None, None, None, 'ta', 'gz')
- action_profile: float32 [128, 32], P('ta', 'gz')
- action_mean: float32 [], replicated
Inputs may be any that keep to these rules, and one draw needn't show every extreme that they name: `time_links`: every 3 x 3 complex matrix is unitary up to float32 rounding. `space_links`: every 3 x 3 complex matrix is unitary up to float32 rounding.
All inputs are finite; a program needn't handle non-finite values.
Results may differ from a plain program's by a relative error of at most 0.00024.
Values sent between devices are 32-bit elements; how exact they have to be, the bound alone decides.
A program may use at most 64 MiB of HBM per device.

v0:
```python
import jax
import jax.numpy as jnp
from jax import lax
from jax.sharding import Mesh
from jax.sharding import PartitionSpec as P

X = 16
Y = 16
TA = ("ta_0", "ta_1", "ta_2")
TA_GZ = ("ta_0", "ta_1", "ta_2", "gz")


def filled_with(shard, identity):
    return jnp.broadcast_to(jnp.asarray(identity, shard.dtype), shard.shape)


def carried_in(shard, axes, combine, identity):
    before = start = filled_with(shard, identity)
    so_far = shard
    for axis in reversed(axes):
        length, mine = (lax.axis_size(axis), lax.axis_index(axis))
        pieces = lax.all_gather(so_far, axis)
        inside, so_far = (start, start)
        for k in range(length):
            passed = k < mine
            so_far = combine(so_far, pieces[k])
            inside = jnp.where(passed, so_far, inside)
        before = combine(inside, before)
    return before


def from_behind(block, axis, distance):
    devices = range(lax.axis_size(axis))
    route = [((i - distance) % len(devices), i) for i in devices]
    return lax.ppermute(block, axis, route)


def over_axes(shard, axes):
    for axis in axes:
        shard = lax.psum(shard, axis)
    return shard


def complex_product(first_pair, second_pair):
    first_real, first_imag = first_pair
    second_real, second_imag = second_pair
    real_part = jnp.sum(
        first_real[:, :, None] * second_real[None] - first_imag[:, :, None] * second_imag[None],
        axis=1,
    )
    imag_part = jnp.sum(
        first_real[:, :, None] * second_imag[None] + first_imag[:, :, None] * second_real[None],
        axis=1,
    )
    return (real_part, imag_part)


def dagger(matrix_pair):
    return (jnp.swapaxes(matrix_pair[0], 0, 1), -jnp.swapaxes(matrix_pair[1], 0, 1))


def plane_step(matrix_pair, direction):

    def shifted(values):
        leading = values.shape[:-1]
        lattice_grid = values.reshape(leading + (X, Y))
        lattice_grid = jnp.roll(lattice_grid, -1, axis=lattice_grid.ndim - 2 + direction)
        return lattice_grid.reshape(leading + (X * Y,))

    return (shifted(matrix_pair[0]), shifted(matrix_pair[1]))


def upward_z(matrix_pair, upper_layer):
    return (
        jnp.concatenate([matrix_pair[0][..., 1:, :], upper_layer[0]], axis=-2),
        jnp.concatenate([matrix_pair[1][..., 1:, :], upper_layer[1]], axis=-2),
    )


def plaquette_density(link_set, forward_x, forward_y):
    forward_z = [forward_x, forward_y]
    terms = []
    for first_dir, second_dir in ((0, 1), (0, 2), (1, 2)):
        along_first = link_set[first_dir]
        along_second = link_set[second_dir]
        second_moved = plane_step(along_second, first_dir)
        if second_dir < 2:
            first_moved = plane_step(along_first, second_dir)
        else:
            first_moved = forward_z[first_dir]
        loop_matrix = complex_product(
            complex_product(along_first, second_moved),
            complex_product(dagger(first_moved), dagger(along_second)),
        )
        trace_real = loop_matrix[0][0, 0] + loop_matrix[0][1, 1] + loop_matrix[0][2, 2]
        terms.append(1.0 - trace_real / 3.0)
    return terms[0] + terms[1] + terms[2]


def on_device(time_links, space_links):
    local_steps = time_links.shape[3]
    layer_count = time_links.shape[4]
    site_count = time_links.shape[5]
    unit_matrix = jnp.eye(3, dtype=jnp.float32)[:, :, None, None]
    unit_real = jnp.broadcast_to(unit_matrix, (3, 3, layer_count, site_count))
    running = (unit_real, jnp.zeros_like(unit_real))
    prefixes = []
    for step_index in range(local_steps):
        prefixes.append(running)
        running = complex_product(
            running, (time_links[0, :, :, step_index], time_links[1, :, :, step_index])
        )

    def combine(earlier, later):
        return jnp.stack(complex_product((earlier[0], earlier[1]), (later[0], later[1])))

    identity_pair = jnp.stack([unit_real, jnp.zeros_like(unit_real)])
    carried = carried_in(jnp.stack(running), TA, combine, identity_pair)
    carried_pair = (carried[0], carried[1])
    time_slices = [complex_product(carried_pair, prefix_pair) for prefix_pair in prefixes]
    gauge_pair = (
        jnp.stack([piece[0] for piece in time_slices], axis=2),
        jnp.stack([piece[1] for piece in time_slices], axis=2),
    )
    first_layer = jnp.stack([gauge_pair[0][..., 0:1, :], gauge_pair[1][..., 0:1, :]])
    gauge_above = from_behind(first_layer, "gz", -1)
    gauge_next_z = upward_z(gauge_pair, (gauge_above[0], gauge_above[1]))
    fixed = []
    for direction in range(3):
        link_pair = (space_links[direction, 0], space_links[direction, 1])
        ahead = plane_step(gauge_pair, direction) if direction < 2 else gauge_next_z
        fixed.append(complex_product(complex_product(gauge_pair, link_pair), dagger(ahead)))
    links_fixed = jnp.stack([jnp.stack(pair) for pair in fixed])
    top_layers = jnp.stack(
        [jnp.stack([pair[0][..., 0:1, :], pair[1][..., 0:1, :]]) for pair in fixed[:2]]
    )
    layers_above = from_behind(top_layers, "gz", -1)
    forward_x = upward_z(fixed[0], (layers_above[0, 0], layers_above[0, 1]))
    forward_y = upward_z(fixed[1], (layers_above[1, 0], layers_above[1, 1]))
    density = plaquette_density(fixed, forward_x, forward_y)
    action_profile = jnp.mean(density, axis=-1) / 3.0
    local_total = jnp.sum(action_profile)
    whole_total = over_axes(local_total, TA_GZ)
    action_mean = whole_total / (action_profile.size * lax.axis_size(TA) * lax.axis_size("gz"))
    return (jnp.stack(gauge_pair), links_fixed, action_profile, action_mean)


def solution(mesh):
    finer = Mesh(mesh.devices.reshape(8, 4, 2, mesh.shape["gz"]), ("ta_0", "ta_1", "ta_2", "gz"))
    placed = (P(None, None, None, TA, "gz", None), P(None, None, None, None, TA, "gz", None))
    return jax.shard_map(
        on_device,
        mesh=finer,
        in_specs=placed,
        out_specs=(
            P(None, None, None, TA, "gz", None),
            P(None, None, None, None, TA, "gz", None),
            P(TA, "gz"),
            P(),
        ),
        check_vma=False,
    )
```

profile of v0, /device:TPU:8, one launch (start us, length us, event | category | flops | bytes accessed | tf_op | source)
XLA Modules:
  0.0 155.2 jit_solution(9629887027639376099)
XLA Ops:
  0.6 0.9 broadcast_multiply_fusion.10
  1.9 1.9 %all-gather = f32[4,3,3,4,256]{4,3,2,1,0:T(4,128)S(1)} all-gather(f32[2,3,3,4,256]{4,3,2,1,0:T(4,128)S(1)} %pad_maximum_fusion.13), channel_id=2, replica_groups=mesh['ta_0'=8,'ta_1'=4,'ta_2'=2,'gz'=8] {'ta_2'}, dimensions={0}, use_global_device_ids=true | all-gather | bytes 221184 | tf_op jit(solution)/shard_map/all_gather | solution.py:22
  4.2 12.7 %all-gather.1 = f32[8,3,3,4,256]{4,3,2,1,0:T(4,128)S(1)} all-gather(f32[2,3,3,4,256]{4,3,2,1,0:T(4,128)S(1)} %get-tuple-element.165), channel_id=3, replica_groups=mesh['ta_0'=8,'ta_1'=4,'ta_2'=2,'gz'=8] {'ta_1'}, dimensions={0}, use_global_device_ids=true | all-gather | bytes 368640 | tf_op jit(solution)/shard_map/all_gather | solution.py:22
  17.4 28.1 %all-gather.2 = f32[16,3,3,4,256]{4,3,2,1,0:T(4,128)S(1)} all-gather(f32[2,3,3,4,256]{4,3,2,1,0:T(4,128)S(1)} %get-tuple-element.159), channel_id=4, replica_groups=mesh['ta_0'=8,'ta_1'=4,'ta_2'=2,'gz'=8] {'ta_0'}, dimensions={0}, use_global_device_ids=true | all-gather | bytes 663552 | tf_op jit(solution)/shard_map/all_gather | solution.py:22
  47.2 0.6 pad_maximum_fusion.17
  47.8 9.2 %collective-permute-start = (f32[2,3,3,2,1,256]{5,3,2,1,4,0:T(2,128)}, f32[2,3,3,2,1,256]{5,3,2,1,4,0:T(2,128)}, u32[]{:S(2)}, u32[]{:S(2)}) collective-permute-start(f32[2,3,3,2,1,256]{5,3,2,1,4,0:T(2,128)} %pad_maximum_fusion.17), channel_id=1, source_target_pairs={{1,0},{2,1},{3,2},{4,3},{5,4},{6,5},{7,6},{0,7},{9,8},{10,9},{11,1... | collective-permute-start | bytes 110600 | tf_op jit(solution)/shard_map/ppermute | solution.py:35
  57.0 0.7 pad_maximum_fusion.12
  57.7 0.7 fusion.30
  59.2 0.6 slice.491
  60.2 0.6 slice.489
  60.9 1.0 copy-done.3
  62.1 0.9 neg.62
  63.0 1.5 copy.214
  64.7 0.3 reshape.231
  65.1 0.7 copy-done.26
  65.9 0.3 neg.59
  66.2 0.7 copy-done.27
  67.1 0.3 reshape.230
  67.4 0.9 copy-done.7
  68.3 1.2 subtract_reduce_fusion.14
  70.1 0.7 pad_maximum_fusion.16
  70.7 2.6 %collective-permute-start.1 = (f32[2,2,3,3,2,1,256]{6,5,4,3,2,1,0:T(1,128)}, f32[2,2,3,3,2,1,256]{6,5,4,3,2,1,0:T(1,128)}, u32[]{:S(2)}, u32[]{:S(2)}) collective-permute-start(f32[2,2,3,3,2,1,256]{6,5,4,3,2,1,0:T(1,128)} %pad_maximum_fusion.16), channel_id=1, source_target_pairs={{1,0},{2,1},{3,2},{4,3},{5,4},{6,5},{7,6},{0,7},{9,8},{10,9},{11,1... | collective-permute-start | bytes 221192 | tf_op jit(solution)/shard_map/ppermute | solution.py:35
  73.4 0.6 fusion.1
  74.3 0.6 slice.509
  75.2 0.6 slice.507
  76.8 0.3 neg.67
  77.1 0.6 copy.212
  78.5 0.9 copy-done.16
  79.4 0.7 pad_maximum_fusion.10
  80.1 0.7 maximum_bitcast_fusion
  81.0 0.7 copy-done.25
  81.7 0.8 copy-done.15
  82.5 0.8 subtract_reduce_fusion.7
  83.4 0.6 slice.536
  84.0 0.7 slice.538
  84.7 0.7 slice.521
  85.4 0.7 slice.527
  86.0 0.9 mul.1834
  86.9 0.9 mul.1830
  87.8 0.7 slice_bitcast_fusion.53
  88.7 0.8 copy-done.5
  89.8 0.6 negate_bitcast_fusion
  91.1 0.6 slice.518
  91.7 0.9 slice.517
  92.8 0.6 slice.520
  93.7 0.9 mul.1880
  95.2 0.8 copy-done
  96.3 0.5 copy-done.28
  97.2 0.6 copy-done.20
  98.0 0.7 copy-done.11
  98.7 0.4 subtract_reduce_fusion.8
  99.1 0.5 copy-done.18
  99.8 0.8 slice_bitcast_fusion.45
  100.7 0.8 copy-done.22
  101.6 0.8 copy-done.21
  102.4 0.8 copy-done.9
  103.3 0.6 subtract_reduce_fusion.4
  104.2 1.2 fusion.29
  105.4 16.0 %psum.28 = f32[]{:T(128)} all-reduce(f32[]{:T(128)} %get-tuple-element.98), channel_id=1, replica_groups=mesh['ta_0'=8,'ta_1'=4,'ta_2'=2,'gz'=8] {'ta_0'}, use_global_device_ids=true, to_apply=%region_71.72 | all-reduce | flops 1 | bytes 8 | tf_op jit(solution)/shard_map/psum | solution.py:40
  121.4 0.7 copy.175
  122.1 11.1 %psum.29 = f32[]{:T(128)} all-reduce(f32[]{:T(128)} %psum.28), channel_id=1, replica_groups=mesh['ta_0'=8,'ta_1'=4,'ta_2'=2,'gz'=8] {'ta_1'}, use_global_device_ids=true, to_apply=%region_72.73 | all-reduce | flops 1 | bytes 8 | tf_op jit(solution)/shard_map/psum | solution.py:40
  133.2 3.1 %psum.30 = f32[]{:T(128)} all-reduce(f32[]{:T(128)} %psum.29), channel_id=1, replica_groups=mesh['ta_0'=8,'ta_1'=4,'ta_2'=2,'gz'=8] {'ta_2'}, use_global_device_ids=true, to_apply=%region_73.74 | all-reduce | flops 1 | bytes 8 | tf_op jit(solution)/shard_map/psum | solution.py:40
  136.3 0.9 pad_maximum_fusion.9
  137.2 16.2 %psum.31 = f32[]{:T(128)} all-reduce(f32[]{:T(128)} %psum.30), channel_id=1, replica_groups=mesh['ta_0'=8,'ta_1'=4,'ta_2'=2,'gz'=8] {'gz'}, use_global_device_ids=true, to_apply=%region_74.75 | all-reduce | flops 1 | bytes 8 | tf_op jit(solution)/shard_map/psum | solution.py:40
  (157 shorter events, 11.4 us)
Async XLA Ops:
  0.6 0.9 copy-start.4
  47.8 40.0 %collective-permute-start = (f32[2,3,3,2,1,256]{5,3,2,1,4,0:T(2,128)}, f32[2,3,3,2,1,256]{5,3,2,1,4,0:T(2,128)}, u32[]{:S(2)}, u32[]{:S(2)}) collective-permute-start(f32[2,3,3,2,1,256]{5,3,2,1,4,0:T(2,128)} %pad_maximum_fusion.17), channel_id=1, source_target_pairs={{1,0},{2,1},{3,2},{4,3},{5,4},{6,5},{7,6},{0,7},{9,8},{10,9},{11,1... | collective-permute-start | bytes 110600 | tf_op jit(solution)/shard_map/ppermute | solution.py:35
  60.8 1.0 copy-start.3
  65.0 0.8 copy-start.26
  66.2 0.8 copy-start.27
  67.4 0.9 copy-start.7
  67.4 0.9 copy-start.8
  68.3 1.2 copy-start.14
  70.7 29.0 %collective-permute-start.1 = (f32[2,2,3,3,2,1,256]{6,5,4,3,2,1,0:T(1,128)}, f32[2,2,3,3,2,1,256]{6,5,4,3,2,1,0:T(1,128)}, u32[]{:S(2)}, u32[]{:S(2)}) collective-permute-start(f32[2,2,3,3,2,1,256]{6,5,4,3,2,1,0:T(1,128)} %pad_maximum_fusion.16), channel_id=1, source_target_pairs={{1,0},{2,1},{3,2},{4,3},{5,4},{6,5},{7,6},{0,7},{9,8},{10,9},{11,1... | collective-permute-start | bytes 221192 | tf_op jit(solution)/shard_map/ppermute | solution.py:35
  78.4 0.9 copy-start.16
  78.4 0.9 copy-start.17
  80.1 0.8 copy-start.24
  80.9 0.8 copy-start.25
  81.6 0.9 copy-start.15
  86.9 1.8 %copy-start.13 = (f32[3,3,2,3,256]{4,3,1,0,2:T(4,128)S(1)}, f32[3,3,2,3,256]{4,3,1,0,2:T(4,128)}, u32[]{:S(2)}) copy-start(f32[3,3,2,3,256]{4,3,1,0,2:T(4,128)} %fusion.1) | copy-start | bytes 165892
  88.6 0.9 copy-start.5
  88.6 0.9 copy-start.6
  94.9 1.1 copy-start
  94.9 1.1 copy-start.29
  96.0 0.8 copy-start.28
  96.9 0.9 copy-start.20
  97.8 0.9 copy-start.11
  97.8 0.9 copy-start.12
  98.7 0.9 copy-start.18
  98.7 0.9 copy-start.19
  99.7 0.9 copy-start.23
  100.6 0.9 copy-start.22
  101.5 0.9 copy-start.21
  102.4 0.9 copy-start.9
  102.4 0.9 copy-start.10
  104.0 17.4 %copy-start.2 = (f32[2,3,3,2,4,256]{5,4,2,1,3,0:T(4,128)S(1)}, f32[2,3,3,2,4,256]{5,4,2,1,3,0:T(4,128)}, u32[]{:S(2)}) copy-start(f32[2,3,3,2,4,256]{5,4,2,1,3,0:T(4,128)} %pad_maximum_fusion.10) | copy-start | bytes 442372
  133.2 3.2 %copy-start.1 = (f32[1,2,3,3,2,4,256]{6,5,4,3,2,1,0:T(4,128)S(1)}, f32[1,2,3,3,2,4,256]{6,5,4,3,2,1,0:T(4,128)}, u32[]{:S(2)}) copy-start(f32[1,2,3,3,2,4,256]{6,5,4,3,2,1,0:T(4,128)} %maximum_bitcast_fusion) | copy-start | bytes 442372
where the time goes:
time: 156 us; the launch traced here: 155 us
  blocking collectives  89.2 us (57%)
  local copies, waits for them, and re-layouts  33.9 us (22%)
  other arithmetic  17.1 us (11%)
  starting transfers between devices  11.8 us (8%)
  between operations  3.22 us (2%)
    psum x4, blocking collectives, over_axes(): shard = lax.psum(shard, axis)  46.5 us
    all_gather x3, blocking collectives, carried_in(): pieces = lax.all_gather(so_far, axis)  42.7 us
    unnamed x63, local copies, waits for them, and re-layouts  13.1 us
    ppermute x2, starting transfers between devices, from_behind(): return lax.ppermute(block, axis, route)  11.8 us
    slice x18, local copies, waits for them, and re-layouts, shifted(): jnp.roll(lattice_grid, -1, axis=lattice_grid.ndim - 2 + direction)  6.19 us
    reduce_sum x29, other arithmetic, complex_product(): jnp.sum(first_real[:, :, None] * second_real[None] - first_imag[:, :, Non...  6.1 us
    neg x6, local copies, waits for them, and re-layouts, dagger(): -jnp.swapaxes(matrix_pair[1], 0, 1)  3.62 us
  transfers between devices with their start and end apart: 2, of which 0 were waited for; matrix products, arithmetic and copies ran while one was open for 19% of the time, Pallas kernels for 0%

commit v1 on v0

--- a/solution.py
+++ b/solution.py
@@ -37,7 +37,7 @@
 
 def over_axes(shard, axes):
     for axis in axes:
-        shard = lax.psum(shard, axis)
+        shard = jnp.sum(lax.all_gather(shard, axis), axis=0)
     return shard
 
 

time: 156 us -> 167 us (1.071)
  local copies, waits for them, and re-layouts: 33.9 us -> 44.6 us
  blocking collectives: 89.2 us -> 86.6 us
  other arithmetic: 17.1 us -> 18.9 us
    psum x4 -> x0, blocking collectives: 46.5 us -> none  [over_axes(): shard = lax.psum(shard, axis)]
    unnamed x0 -> x4, blocking collectives: none -> 43.9 us
    unnamed x63 -> x73, local copies, waits for them, and re-layouts: 13.1 us -> 23.9 us
    reduce_sum x0 -> x4, other arithmetic: none -> 2.41 us  [over_axes(): shard = jnp.sum(lax.all_gather(shard, axis), axis=0)]
  transfers between devices with their start and end apart: 2 -> 2, of which waited for: 0 -> 0; matrix products, arithmetic and copies ran while one was open for 19% -> 20% of each run, Pallas kernels for 0% -> 0%
where the time goes in v1:
time: 167 us; the launch traced here: 165 us
  blocking collectives  86.6 us (52%)
  local copies, waits for them, and re-layouts  44.6 us (27%)
  other arithmetic  18.9 us (11%)
  starting transfers between devices  11.8 us (7%)
  between operations  3.22 us (2%)
    unnamed x4, blocking collectives  43.9 us
    all_gather x3, blocking collectives, carried_in(): pieces = lax.all_gather(so_far, axis)  42.7 us
    unnamed x73, local copies, waits for them, and re-layouts  23.9 us
    ppermute x2, starting transfers between devices, from_behind(): return lax.ppermute(block, axis, route)  11.8 us
    slice x18, local copies, waits for them, and re-layouts, shifted(): jnp.roll(lattice_grid, -1, axis=lattice_grid.ndim - 2 + direction)  6.17 us
    reduce_sum x29, other arithmetic, complex_product(): jnp.sum(first_real[:, :, None] * second_real[None] - first_imag[:, :, Non...  6.1 us
    neg x6, local copies, waits for them, and re-layouts, dagger(): -jnp.swapaxes(matrix_pair[1], 0, 1)  3.64 us
  transfers between devices with their start and end apart: 2, of which 0 were waited for; matrix products, arithmetic and copies ran while one was open for 20% of the time, Pallas kernels for 0%

profile of v1, /device:TPU:8, one launch (start us, length us, event | category | flops | bytes accessed | tf_op | source)
XLA Modules:
  0.0 165.2 jit_solution(12926302872175895109)
XLA Ops:
  0.6 0.9 broadcast_multiply_fusion.10
  1.9 1.9 %all-gather = f32[4,3,3,4,256]{4,3,2,1,0:T(4,128)S(1)} all-gather(f32[2,3,3,4,256]{4,3,2,1,0:T(4,128)S(1)} %pad_maximum_fusion.13), channel_id=2, replica_groups=mesh['ta_0'=8,'ta_1'=4,'ta_2'=2,'gz'=8] {'ta_2'}, dimensions={0}, use_global_device_ids=true | all-gather | bytes 221184 | tf_op jit(solution)/shard_map/all_gather | solution.py:22
  4.2 12.7 %all-gather.1 = f32[8,3,3,4,256]{4,3,2,1,0:T(4,128)S(1)} all-gather(f32[2,3,3,4,256]{4,3,2,1,0:T(4,128)S(1)} %get-tuple-element.165), channel_id=3, replica_groups=mesh['ta_0'=8,'ta_1'=4,'ta_2'=2,'gz'=8] {'ta_1'}, dimensions={0}, use_global_device_ids=true | all-gather | bytes 368640 | tf_op jit(solution)/shard_map/all_gather | solution.py:22
  17.4 28.1 %all-gather.2 = f32[16,3,3,4,256]{4,3,2,1,0:T(4,128)S(1)} all-gather(f32[2,3,3,4,256]{4,3,2,1,0:T(4,128)S(1)} %get-tuple-element.159), channel_id=4, replica_groups=mesh['ta_0'=8,'ta_1'=4,'ta_2'=2,'gz'=8] {'ta_0'}, dimensions={0}, use_global_device_ids=true | all-gather | bytes 663552 | tf_op jit(solution)/shard_map/all_gather | solution.py:22
  47.2 0.6 pad_maximum_fusion.17
  47.8 9.2 %collective-permute-start = (f32[2,3,3,2,1,256]{5,3,2,1,4,0:T(2,128)}, f32[2,3,3,2,1,256]{5,3,2,1,4,0:T(2,128)}, u32[]{:S(2)}, u32[]{:S(2)}) collective-permute-start(f32[2,3,3,2,1,256]{5,3,2,1,4,0:T(2,128)} %pad_maximum_fusion.17), channel_id=1, source_target_pairs={{1,0},{2,1},{3,2},{4,3},{5,4},{6,5},{7,6},{0,7},{9,8},{10,9},{11,1... | collective-permute-start | bytes 110600 | tf_op jit(solution)/shard_map/ppermute | solution.py:35
  57.0 0.7 pad_maximum_fusion.12
  57.7 0.7 fusion.30
  59.2 0.6 slice.491
  60.2 0.6 slice.489
  60.9 1.0 copy-done.2
  62.1 0.9 neg.62
  63.0 1.5 copy.214
  65.0 0.7 copy-done.25
  66.2 0.7 copy-done.26
  67.4 0.9 copy-done.6
  68.3 1.2 subtract_reduce_fusion.14
  70.0 0.7 pad_maximum_fusion.16
  70.7 2.6 %collective-permute-start.1 = (f32[2,2,3,3,2,1,256]{6,5,4,3,2,1,0:T(1,128)}, f32[2,2,3,3,2,1,256]{6,5,4,3,2,1,0:T(1,128)}, u32[]{:S(2)}, u32[]{:S(2)}) collective-permute-start(f32[2,2,3,3,2,1,256]{6,5,4,3,2,1,0:T(1,128)} %pad_maximum_fusion.16), channel_id=1, source_target_pairs={{1,0},{2,1},{3,2},{4,3},{5,4},{6,5},{7,6},{0,7},{9,8},{10,9},{11,1... | collective-permute-start | bytes 221192 | tf_op jit(solution)/shard_map/ppermute | solution.py:35
  73.4 0.7 fusion.1
  74.3 0.6 slice.509
  75.2 0.6 slice.507
  77.1 0.6 copy.212
  78.5 0.9 copy-done.15
  79.5 0.7 maximum_bitcast_fusion
  80.3 0.7 copy-done.24
  81.1 0.8 copy-done.14
  81.9 0.8 subtract_reduce_fusion.7
  82.7 0.6 slice.536
  83.4 0.7 slice.538
  84.0 0.7 slice.521
  84.7 0.7 slice.527
  85.3 0.7 copy.175
  86.0 0.9 mul.1834
  86.9 0.9 mul.1830
  87.9 1.3 dynamic-slice
  89.2 1.3 dynamic-slice.1
  90.5 0.7 slice_bitcast_fusion.53
  91.3 0.8 copy-done.4
  92.4 0.6 negate_bitcast_fusion
  93.7 0.6 slice.518
  94.4 0.9 slice.517
  95.4 0.6 slice.520
  96.4 0.9 mul.1880
  97.8 0.8 copy-done
  100.6 0.7 copy-done.10
  102.4 0.8 slice_bitcast_fusion.45
  103.3 0.8 copy-done.21
  104.2 0.8 copy-done.20
  105.1 0.8 copy-done.8
  106.8 1.2 fusion.29
  108.0 1.4 dynamic-update-slice
  109.4 1.3 dynamic-slice.2
  110.7 15.4 %all-reduce.1 = f32[8]{0:T(128)S(1)} all-reduce(f32[8]{0:T(128)S(1)} %dynamic-update-slice), channel_id=1, replica_groups=mesh['ta_0'=8,'ta_1'=4,'ta_2'=2,'gz'=8] {'ta_0'}, use_global_device_ids=true, to_apply=%add.1 | all-reduce | flops 8 | bytes 64
  126.1 0.6 reduce_sum.746
  126.7 1.4 dynamic-update-slice.1
  128.1 1.3 dynamic-slice.3
  129.3 10.5 %all-reduce.2 = f32[4]{0:T(128)S(1)} all-reduce(f32[4]{0:T(128)S(1)} %dynamic-update-slice.1), channel_id=1, replica_groups=mesh['ta_0'=8,'ta_1'=4,'ta_2'=2,'gz'=8] {'ta_1'}, use_global_device_ids=true, to_apply=%add.2 | all-reduce | flops 4 | bytes 32
  139.8 0.6 reduce_sum.747
  140.4 1.4 dynamic-update-slice.2
  141.9 2.5 %all-reduce.3 = f32[2]{0:T(128)S(1)} all-reduce(f32[2]{0:T(128)S(1)} %dynamic-update-slice.2), channel_id=1, replica_groups=mesh['ta_0'=8,'ta_1'=4,'ta_2'=2,'gz'=8] {'ta_2'}, use_global_device_ids=true, to_apply=%add.3 | all-reduce | flops 2 | bytes 16
  145.0 1.3 dynamic-update-slice.3
  146.3 0.9 pad_maximum_fusion.9
  147.2 15.6 %all-reduce.4 = f32[8]{0:T(128)S(1)} all-reduce(f32[8]{0:T(128)S(1)} %dynamic-update-slice.3), channel_id=1, replica_groups=mesh['ta_0'=8,'ta_1'=4,'ta_2'=2,'gz'=8] {'gz'}, use_global_device_ids=true, to_apply=%add.4 | all-reduce | flops 8 | bytes 64
  (171 shorter events, 16.4 us)
Async XLA Ops:
  0.6 0.9 copy-start.3
  47.8 42.6 %collective-permute-start = (f32[2,3,3,2,1,256]{5,3,2,1,4,0:T(2,128)}, f32[2,3,3,2,1,256]{5,3,2,1,4,0:T(2,128)}, u32[]{:S(2)}, u32[]{:S(2)}) collective-permute-start(f32[2,3,3,2,1,256]{5,3,2,1,4,0:T(2,128)} %pad_maximum_fusion.17), channel_id=1, source_target_pairs={{1,0},{2,1},{3,2},{4,3},{5,4},{6,5},{7,6},{0,7},{9,8},{10,9},{11,1... | collective-permute-start | bytes 110600 | tf_op jit(solution)/shard_map/ppermute | solution.py:35
  60.8 1.0 copy-start.2
  65.0 0.8 copy-start.25
  66.2 0.8 copy-start.26
  67.4 0.9 copy-start.6
  67.4 0.9 copy-start.7
  68.3 1.2 copy-start.13
  70.7 31.6 %collective-permute-start.1 = (f32[2,2,3,3,2,1,256]{6,5,4,3,2,1,0:T(1,128)}, f32[2,2,3,3,2,1,256]{6,5,4,3,2,1,0:T(1,128)}, u32[]{:S(2)}, u32[]{:S(2)}) collective-permute-start(f32[2,2,3,3,2,1,256]{6,5,4,3,2,1,0:T(1,128)} %pad_maximum_fusion.16), channel_id=1, source_target_pairs={{1,0},{2,1},{3,2},{4,3},{5,4},{6,5},{7,6},{0,7},{9,8},{10,9},{11,1... | collective-permute-start | bytes 221192 | tf_op jit(solution)/shard_map/ppermute | solution.py:35
  78.4 0.9 copy-start.15
  78.4 0.9 copy-start.16
  79.4 0.8 copy-start.23
  80.2 0.8 copy-start.24
  81.0 0.9 copy-start.14
  86.9 4.4 %copy-start.12 = (f32[3,3,2,3,256]{4,3,1,0,2:T(4,128)S(1)}, f32[3,3,2,3,256]{4,3,1,0,2:T(4,128)}, u32[]{:S(2)}) copy-start(f32[3,3,2,3,256]{4,3,1,0,2:T(4,128)} %fusion.1) | copy-start | bytes 165892
  91.3 0.9 copy-start.4
  91.3 0.9 copy-start.5
  97.5 1.1 copy-start
  97.5 1.1 copy-start.28
  98.7 0.8 copy-start.27
  99.5 0.9 copy-start.19
  100.4 0.9 copy-start.10
  100.4 0.9 copy-start.11
  101.3 0.9 copy-start.17
  101.3 0.9 copy-start.18
  102.4 0.9 copy-start.22
  103.3 0.9 copy-start.21
  104.1 0.9 copy-start.20
  105.0 0.9 copy-start.8
  105.0 0.9 copy-start.9
  141.9 4.4 %copy-start.1 = (f32[1,2,3,3,2,4,256]{6,5,4,3,2,1,0:T(4,128)S(1)}, f32[1,2,3,3,2,4,256]{6,5,4,3,2,1,0:T(4,128)}, u32[]{:S(2)}) copy-start(f32[1,2,3,3,2,4,256]{6,5,4,3,2,1,0:T(4,128)} %maximum_bitcast_fusion) | copy-start | bytes 442372
